TPU v7x, 32 devices: a whole 2x2x4 slice. The times are simulated.
32 devices in a mesh: groups: 2 (over x), dom: 16 (over z, y, core).
Axes of the slice: x: 2, y: 2, z: 4, core: 2. Of those that a mesh axis runs over, the one named last changes fastest.
Arguments:
- node_latent: bfloat16 [32768, 128], P(('groups', 'dom')), parts along dimension 0, may hold values from -6 to 6
- edge_latent: bfloat16 [196608, 128], P(('groups', 'dom')), parts along dimension 0, may hold values from -6 to 6
- node_cot: bfloat16 [32768, 128], P(('groups', 'dom')), parts along dimension 0, may hold values from -6 to 6
- edge_cot: bfloat16 [196608, 128], P(('groups', 'dom')), parts along dimension 0, may hold values from -6 to 6
- base_pos: float32 [3, 32768], P(None, ('groups', 'dom')), parts along dimension 1
- centers: float32 [3, 2048], replicated, may hold values from 0 to 1
- amplitudes: float32 [3, 2048], replicated, may hold values from -0.3 to 0.3
- edge_in: bfloat16 [384, 128], replicated, may hold values from -0.3125 to 0.3125
- edge_geo: float32 [4, 128], replicated, may hold values from -3 to 3
- edge_out: bfloat16 [128, 128], replicated, may hold values from -0.5 to 0.5
- edge_gain: float32 [128], replicated, may hold values from 0.5 to 1.5
- node_in: bfloat16 [256, 128], replicated, may hold values from -0.375 to 0.375
- node_out: bfloat16 [128, 128], replicated, may hold values from -0.5 to 0.5
- node_gain: float32 [128], replicated, may hold values from 0.5 to 1.5
- senders: int32 [196608], P(('groups', 'dom')), parts along dimension 0, may hold values from 0 to 3071, as said below
- receivers: int32 [196608], P(('groups', 'dom')), parts along dimension 0, may hold values from 0 to 1023
- send_rows: int32 [32, 16, 128], P(('groups', 'dom')), parts along dimension 0, may hold values from 0 to 1023
Outputs:
- grad_nodes: float32 [32768, 128], P(('groups', 'dom')), parts along dimension 0
- grad_edges: float32 [196608, 128], P(('groups', 'dom')), parts along dimension 0
- grad_controls: float32 [6, 2048], P('groups'), parts along dimension 0
There are 2 independent parts, one for each index of `groups`. A program takes and returns all parts, laid end to end along the dimension named above; an argument that names none is the same for every part. Nothing has to cross between parts.
Inputs may be any that keep to these rules, and one draw needn't show every extreme that they name: `senders`: for edge j in partition q = j // 6144: a value below 1024 is an own node; a value v of 1024 or more names slot (v - 1024) % 128 of the block from partition p = (v - 1024) // 128, and 1 <= |p - q| <= 2. Every partition has an edge using slot 127 of some block.
All inputs are finite; a program needn't handle non-finite values.
Results may differ from a plain program's by a relative error of at most 0.0085.
Values may be sent and summed in bfloat16 or wider, within the bound.
A program may use at most 128 MiB of HBM per device.

v0:
```python
import functools

import jax
import jax.numpy as jnp
from jax import lax
from jax.experimental import pallas as pl
from jax.experimental.pallas import tpu as pltpu
from jax.sharding import PartitionSpec as P

REACH = 2
RBF_RATE = 78.125
SCALE = (RBF_RATE * 1.4426950408889634) ** 0.5
FAR = 4.0 * SCALE
OFFSETS = [step for step in range(-REACH, REACH + 1) if step != 0]
NEAR = len(OFFSETS)
F32 = jnp.float32
BF16 = jnp.bfloat16
LANES = 128
VMEM_FULL = pl.BlockSpec(memory_space=pltpu.VMEM)
ANY = pl.BlockSpec(memory_space=pl.ANY)


def dot(a, b):
    return jnp.dot(a, b, preferred_element_type=F32)


def dot_t(a, b):
    return lax.dot_general(a, b, (((1,), (1,)), ((), ())), preferred_element_type=F32)


def stack_rows(rows, height):
    at = lax.broadcasted_iota(jnp.int32, (height, rows[0].shape[1]), 0)
    out = jnp.zeros(at.shape, F32)
    for k, row in enumerate(rows):
        if row is not None:
            out = jnp.where(at == k, row, out)
    return out


def split(x):
    hi = x.astype(BF16)
    return hi, (x - hi.astype(F32)).astype(BF16)


def three(x):
    hi = x.astype(BF16).astype(F32)
    rest = x - hi
    mid = rest.astype(BF16).astype(F32)
    return hi, mid, rest - mid


def as_columns(row):
    wide = jnp.broadcast_to(row.astype(F32), (LANES, row.shape[1])).astype(BF16)
    return jnp.transpose(wide)


def lane_iota(shape):
    return lax.broadcasted_iota(jnp.int32, shape, 1).astype(F32).astype(BF16)


def tiles_match(key, count):
    one, zero = jnp.ones_like(key), jnp.zeros_like(key)
    return jnp.concatenate(
        [jnp.where(key == jnp.full_like(key, j), one, zero) for j in range(count)], axis=1
    )


def columns_match(row, width):
    within = as_columns(row % LANES)
    tile = as_columns(row // LANES)
    key = jnp.where(within == lane_iota(within.shape), tile, jnp.full_like(tile, -1.0))
    return tiles_match(key, width // LANES)


def rows_match(row, height):
    block = row.shape[1]
    group = row // 16
    at = lax.broadcasted_iota(jnp.int32, (16, block), 0)
    key = jnp.where(at == row - group * 16, group, -1).astype(F32).astype(BF16)
    one, zero = jnp.ones_like(key), jnp.zeros_like(key)
    return jnp.concatenate(
        [jnp.where(key == jnp.full_like(key, q), one, zero) for q in range(height // 16)], axis=0
    )


def lane_gather(table_ref, row, count):
    block = row.shape[1]
    lane = jnp.broadcast_to(row % LANES, (8, block))
    tile = jnp.broadcast_to(row // LANES, (8, block))
    pieces = []
    for j in range(block // LANES):
        here = slice(j * LANES, (j + 1) * LANES)
        out = jnp.zeros((8, LANES), F32)
        for c in range(count):
            source = table_ref[:, c * LANES : (c + 1) * LANES]
            taken = jnp.take_along_axis(source, lane[:, here], axis=1, mode="promise_in_bounds")
            out = jnp.where(tile[:, here] == c, taken, out)
        pieces.append(out)
    return jnp.concatenate(pieces, axis=1)


def compact_row(raw, nodes, slots):
    me = lax.axis_index("dom")
    slot = jnp.maximum(raw - nodes, 0)
    off = slot // slots - me
    near = jnp.clip(jnp.where(off < 0, off + REACH, off + REACH - 1), 0, NEAR - 1)
    return jnp.where(raw >= nodes, nodes + near * slots + slot % slots, raw)


def neighbours(parts):
    me = lax.axis_index("dom")
    out = []
    for off in OFFSETS:
        there = me + off
        inside = (there >= 0) & (there < parts)
        out.append((inside, lax.rem(there + parts, parts)))
    return out


def remote(src, dst, send_sem, recv_sem, partner):
    return pltpu.make_async_remote_copy(
        src_ref=src,
        dst_ref=dst,
        send_sem=send_sem,
        recv_sem=recv_sem,
        device_id={"dom": partner},
        device_id_type=pl.DeviceIdType.MESH,
    )


def copy_all(pairs, sems):
    copies = [
        pltpu.make_async_copy(source, target, sems.at[i]) for i, (source, target) in enumerate(pairs)
    ]
    for copy in copies:
        copy.start()
    return copies


def normed_of(values):
    centred = values - jnp.mean(values, axis=-1, keepdims=True)
    inv = lax.rsqrt(jnp.mean(centred * centred, axis=-1, keepdims=True) + 1e-05)
    return centred * inv, inv


def norm_back(values, gain, upstream):
    normed, inv = normed_of(values)
    scaled = upstream * gain
    return inv * (
        scaled
        - jnp.mean(scaled, axis=-1, keepdims=True)
        - normed * jnp.mean(scaled * normed, axis=-1, keepdims=True)
    )


def sigmoid(values):
    return 0.5 * jnp.tanh(0.5 * values) + 0.5


def paired(values, weights):
    half = values.shape[0] // 2
    out = dot(jnp.concatenate([values[:half], values[half:]], axis=1), weights)
    return jnp.concatenate([out[:, :LANES], out[:, LANES:]], axis=0)


def picked(pair, second):
    pair = pair.astype(BF16)
    return jnp.where(second, pair[:, LANES:], pair[:, :LANES])


def halves(values, second):
    zero = jnp.zeros_like(values)
    return jnp.concatenate([jnp.where(second, zero, values), jnp.where(second, values, zero)], axis=1)


def layer_kernel(parts, *refs):
    (
        lat_hbm,
        pos_hbm,
        cen_hbm,
        amp_hbm,
        rows_hbm,
        sidx_hbm,
        ridx_hbm,
        ein_hbm,
        egeo_hbm,
        eout_hbm,
        egain_hbm,
        nin_hbm,
        nout_hbm,
        ngain_hbm,
        elat_hbm,
        ecot_hbm,
        ncot_hbm,
        gedge_s,
        out_ref,
        amp_out,
        lat_ref,
        pos_ref,
        cen_ref,
        amp_ref,
        rows_ref,
        sidx_ref,
        ridx_ref,
        ein_ref,
        egeo_ref,
        eout_ref,
        egain_ref,
        nin_ref,
        nout_ref,
        ngain_ref,
        load_sem,
        halo_ref,
        place_ref,
        out_s,
        pout_s,
        pin_s,
        base_s,
        cmat_s,
        phi_s,
        send_sem,
        recv_sem,
        psend_sem,
        precv_sem,
        elat_s,
        ecot_s,
        ncot_s,
        ghid_s,
        gnode_s,
        elat_sem,
        ecot_sem,
        ncot_sem,
        stab_s,
        rtab_s,
        gtab_s,
        win_s,
        wout_s,
        woutt_s,
        wgeo_s,
        wedge_s,
        peer_s,
        wnode_s,
        slope_s,
        normed_s,
        rkey_s,
        rtile_s,
        stile_s,
        unit_s,
        agg_s,
        sgeo_s,
        rgeo_s,
        ctrl_ref,
        sum_s,
        rsum_s,
        back_s,
        got_s,
        part_s,
        mine_s,
        all_s,
        back_send,
        back_recv,
        part_send,
        part_recv,
        all_send,
        all_recv,
    ) = refs
    nodes = lat_ref.shape[0]
    slots = rows_ref.shape[2]
    controls = cen_ref.shape[1]
    partners = neighbours(parts)
    me = lax.axis_index("dom")
    others = [lax.rem(me + i, parts) for i in range(1, parts)]
    sources = [lax.rem(me + parts - i, parts) for i in range(1, parts)]
    barrier = pltpu.get_barrier_semaphore()
    for other in others:
        pl.semaphore_signal(
            barrier, inc=1, device_id={"dom": other}, device_id_type=pl.DeviceIdType.MESH
        )
    loads = copy_all(
        [
            (rows_hbm, rows_ref),
            (lat_hbm, lat_ref),
            (pos_hbm, pos_ref),
            (cen_hbm, cen_ref),
            (amp_hbm, amp_ref),
            (sidx_hbm, sidx_ref),
            (ridx_hbm, ridx_ref),
            (ein_hbm, ein_ref),
            (egeo_hbm, egeo_ref),
            (eout_hbm, eout_ref),
            (egain_hbm, egain_ref),
            (nin_hbm, nin_ref),
            (nout_hbm, nout_ref),
            (ngain_hbm, ngain_ref),
        ],
        load_sem,
    )
    width = lat_ref.shape[1]
    away = NEAR * slots
    every = nodes + away
    turns, _, block = sidx_ref.shape
    shalf = every // 2
    rhalf = nodes // 2

    def rows_of(t):
        return pl.ds(pl.multiple_of(t * block, block), block)

    def elat_copy(t):
        return pltpu.make_async_copy(elat_hbm.at[rows_of(t)], elat_s.at[rows_of(t)], elat_sem.at[t])

    def ecot_copy(t):
        return pltpu.make_async_copy(ecot_hbm.at[rows_of(t)], ecot_s.at[rows_of(t)], ecot_sem.at[t])

    for t in range(turns):
        elat_copy(t).start()
    load_ncot = pltpu.make_async_copy(ncot_hbm, ncot_s, ncot_sem)
    load_ncot.start()
    for t in range(turns):
        ecot_copy(t).start()
    for load in loads[:5]:
        load.wait()
    rows = [rows_ref[0, pl.ds(partner, 1), :] for _, partner in partners]
    base_s[...] = stack_rows([pos_ref[k : k + 1, :] for k in range(3)], 8)
    match = columns_match(jnp.concatenate(rows, axis=1), nodes)
    taken = dot(match, lat_ref[...]).astype(BF16)
    for k in range(NEAR):
        out_s[k] = taken[k * slots : (k + 1) * slots]
        pout_s[k] = lane_gather(base_s, rows[k], nodes // LANES)
    for k, (inside, _) in enumerate(partners):

        @pl.when(jnp.logical_not(inside))
        def _():
            halo_ref[k] = jnp.zeros_like(halo_ref[k])
            pin_s[k] = jnp.zeros_like(pin_s[k])

    def copies(k):
        there = NEAR - 1 - k
        partner = partners[k][1]
        return (
            remote(out_s.at[k], halo_ref.at[there], send_sem.at[k], recv_sem.at[there], partner),
            remote(pout_s.at[k], pin_s.at[there], psend_sem.at[k], precv_sem.at[there], partner),
        )

    cen = [SCALE * (cen_ref[k : k + 1, :] - 0.5) for k in range(3)]
    crows = []
    for k in range(3):
        hi, mid, low = three(cen[k])
        crows += [hi, mid, hi, low, mid, hi]
    ones = jnp.ones_like(cen[0])
    crows += [ones, ones, ones]
    crows += list(three(-(cen[0] * cen[0] + cen[1] * cen[1] + cen[2] * cen[2])))
    cmat_s[...] = jnp.concatenate(
        [stack_rows(crows[j : j + 8], 8) for j in range(0, 24, 8)]
        + [jnp.zeros((LANES - 24, controls), F32)],
        axis=0,
    ).astype(BF16)
    amp = stack_rows([amp_ref[k : k + 1, :] for k in range(3)], 8)
    amp_hi = amp.astype(BF16).astype(F32)
    amp16 = jnp.concatenate([amp_hi, amp - amp_hi], axis=0).astype(BF16)

    def radial(base, first, size, index=0):
        moved = jnp.clip(SCALE * (base - 0.5), -FAR, FAR)
        parts_of = [three(moved[k : k + 1]) for k in range(3)]
        prows = []
        for hi, mid, low in parts_of:
            hi2, mid2, low2 = 2.0 * hi, 2.0 * mid, 2.0 * low
            prows += [hi2, hi2, mid2, hi2, mid2, low2]
        norm = moved[0:1] * moved[0:1] + moved[1:2] * moved[1:2] + moved[2:3] * moved[2:3]
        prows += list(three(-norm))
        one = jnp.ones_like(norm)
        prows += [one, one, one]
        wide = jnp.concatenate(
            [stack_rows(prows[j : j + 8], 8) for j in range(0, 24, 8)]
            + [jnp.zeros((LANES - 24, size), F32)],
            axis=0,
        )
        left = jnp.transpose(wide).astype(BF16)
        phi = jnp.exp2(dot(left, cmat_s[...])).astype(BF16)
        phi_s[pl.ds(first, size), :] = phi
        shift = dot_t(amp16, phi)
        place_ref[:, pl.ds(first, size)] = base + (shift[0:8] + shift[8:16])

    size = 256
    own = nodes // size

    def own_step(i, carry):
        first = pl.multiple_of(i * size, size)
        radial(base_s[:, pl.ds(first, size)], first, size, i)
        return carry

    lax.fori_loop(0, own, own_step, 0)
    pl.semaphore_wait(barrier, parts - 1)

    for k, (inside, _) in enumerate(partners):

        @pl.when(inside)
        def _():
            for copy in copies(k):
                copy.start()

    for load in loads[5:]:
        load.wait()
    agg_s[...] = jnp.zeros_like(agg_s)
    sgeo_s[...] = jnp.zeros_like(sgeo_s)
    rgeo_s[...] = jnp.zeros_like(rgeo_s)
    stab_s[:, :width] = lat_ref[:shalf]
    stab_s[: nodes - shalf, width:] = lat_ref[shalf:]
    rtab_s[:, :width] = lat_ref[:rhalf]
    rtab_s[:, width:] = lat_ref[rhalf:]
    geo = stack_rows([egeo_ref[k : k + 1, :] for k in range(4)], 8)
    hi = geo.astype(BF16).astype(F32)
    win_s[: 3 * width] = ein_ref[...]
    win_s[3 * width :] = jnp.concatenate(
        [hi + pltpu.roll(hi, 4, 0), geo - hi, jnp.zeros((LANES - 16, width), F32)], axis=0
    ).astype(BF16)
    w_out = eout_ref[...]
    zero = jnp.zeros_like(w_out)
    turned = jnp.transpose(w_out.astype(F32)).astype(BF16)
    wout_s[...] = jnp.concatenate(
        [jnp.concatenate([w_out, zero], axis=1), jnp.concatenate([zero, w_out], axis=1)], axis=0
    )
    woutt_s[...] = jnp.concatenate(
        [jnp.concatenate([turned, zero], axis=1), jnp.concatenate([zero, turned], axis=1)],
        axis=0,
    )
    w_edge = jnp.transpose(ein_ref[2 * width :].astype(F32)).astype(BF16)
    third = egeo_ref[3:4, :]
    spread = stack_rows(
        [egeo_ref[k : k + 1, :] for k in range(3)] + [None, third, third, third], 8
    )
    spread = jnp.transpose(jnp.concatenate([spread] * (LANES // 8), axis=0)).astype(BF16)
    w_send = jnp.transpose(ein_ref[:width].astype(F32)).astype(BF16)
    w_recv = jnp.transpose(ein_ref[width : 2 * width].astype(F32)).astype(BF16)
    wnode_s[...] = jnp.concatenate([w_send, w_send, w_recv, w_recv], axis=0)
    wgeo_s[...] = jnp.concatenate(
        [jnp.concatenate([spread, zero], axis=1), jnp.concatenate([zero, spread], axis=1)], axis=0
    )
    wedge_s[...] = jnp.concatenate(
        [jnp.concatenate([w_edge, zero], axis=1), jnp.concatenate([zero, w_edge], axis=1)], axis=0
    )

    def upper_of(tile):
        return tile >= jnp.full_like(tile, rhalf // LANES)

    def receive(t, carry):
        at = rows_of(t)
        rrow = ridx_ref[t]
        rtile = as_columns(rrow // LANES)
        upper = upper_of(rtile)
        local = jnp.where(upper, rtile - jnp.full_like(rtile, rhalf // LANES), rtile)
        none = jnp.full_like(rtile, -1.0)
        rkey = jnp.where(as_columns(rrow % LANES) == lane_iota(rtile.shape), local, none)
        peer_s[at, :] = picked(dot(tiles_match(rkey, rhalf // LANES), rtab_s[...]), upper)
        rtile_s[at, :] = rtile
        rkey_s[at, :] = rkey
        return carry

    lax.fori_loop(0, turns, receive, 0)
    for k, (inside, _) in enumerate(partners):

        @pl.when(inside)
        def _():
            for copy in copies(NEAR - 1 - k):
                copy.wait_recv()

    pair = size // slots
    for j in range(NEAR // pair):
        halo = jnp.concatenate([pin_s[j * pair + i] for i in range(pair)], axis=1)
        radial(halo, nodes + j * size, size, own + j)
    for k in range(NEAR):
        stab_s[nodes - shalf + k * slots : nodes - shalf + (k + 1) * slots, width:] = halo_ref[k]

    sub = 256
    subs = block // sub

    def forward(t, carry):
        srow = compact_row(sidx_ref[t], nodes, slots)
        rrow = ridx_ref[t]
        elat_copy(t).wait()
        delta = lane_gather(place_ref, srow, every // LANES) - lane_gather(
            place_ref, rrow, nodes // LANES
        )
        length = jnp.sqrt(jnp.sum(delta * delta, axis=0, keepdims=True) + 0.01)
        level = lax.broadcasted_iota(jnp.int32, delta.shape, 0)
        geo = jnp.where(level == 3, length, delta)
        hi = geo.astype(BF16).astype(F32)
        wide = jnp.concatenate(
            [hi + pltpu.roll(geo - hi, 4, 0), hi, jnp.zeros((LANES - 16, block), F32)], axis=0
        ).astype(BF16)
        unit = jnp.where(level < 3, 1.0, pltpu.roll(delta * (1.0 / length), 4, 0)).astype(F32)
        unit = jnp.concatenate([unit] * (LANES // 8), axis=0).astype(BF16)
        lane = lane_iota((sub, LANES))
        none = jnp.full_like(lane, -1.0)

        def place_of(c):
            return pl.ds(pl.multiple_of(t * block + c * sub, sub), sub)

        def gathered(c):
            here = slice(c * sub, (c + 1) * sub)
            at = place_of(c)
            stile = as_columns(srow[:, here] // LANES)
            shift = jnp.full_like(stile, shalf // LANES)
            second = stile >= shift
            local = jnp.where(second, stile - shift, stile)
            skey = jnp.where(as_columns(srow[:, here] % LANES) == lane, local, none)
            sent = picked(dot(tiles_match(skey, shalf // LANES), stab_s[...]), second)
            stile_s[at, :] = stile
            unit_s[at, :] = jnp.transpose(unit[:, here])
            return jnp.concatenate(
                [sent, peer_s[at, :], elat_s[at, :], jnp.transpose(wide[:, here])], axis=1
            )

        def middle(c, joined):
            at = place_of(c)
            pre = dot(joined, win_s[...])
            sigma = sigmoid(pre)
            hidden = pre * sigma
            slope = sigma + hidden * (1.0 - sigma)
            normed, inv = normed_of(paired(hidden.astype(BF16), wout_s[...]))
            slope_s[at, :] = slope * inv
            normed_s[at, :] = normed
            latent = joined[:, 2 * width : 3 * width]
            updated = (latent.astype(F32) + normed * egain_ref[...]).astype(BF16)
            return halves(updated, upper_of(rtile_s[at, :]))

        joined = [None] * subs
        added = [None] * subs
        joined[0] = gathered(0)
        for c in range(1, subs + 1):
            if c < subs:
                joined[c] = gathered(c)
            added[c - 1] = middle(c - 1, joined[c - 1])
            joined[c - 1] = None
        group = 4
        for g in range(0, subs, group):
            row = rrow[:, g * sub : (g + group) * sub] % rhalf
            agg_s[...] += dot(rows_match(row, rhalf), jnp.concatenate(added[g : g + group], axis=0))
        return carry

    lax.fori_loop(0, turns, forward, 0)
    load_ncot.wait()
    latent = lat_ref[...]
    w_node = nin_ref[:width, :]
    w_agg = nin_ref[width:, :]
    cot = ncot_s[...].astype(F32)
    agg = jnp.concatenate([agg_s[:, :width], agg_s[:, width:]], axis=0).astype(BF16)
    node_pre = dot(jnp.concatenate([latent, agg], axis=1), nin_ref[...])
    sigma = sigmoid(node_pre)
    hidden = node_pre * sigma
    node_mid = dot(hidden.astype(BF16), nout_ref[...])
    grad_mid = norm_back(node_mid, ngain_ref[...], cot).astype(BF16)
    grad_pre = (
        dot_t(grad_mid, nout_ref[...]) * (sigma + hidden * (1.0 - sigma))
    ).astype(BF16)
    gagg = dot_t(grad_pre, w_agg).astype(BF16)
    gtab_s[...] = jnp.concatenate([gagg[:rhalf], gagg[rhalf:]], axis=1)
    gnode_s[...] = cot + dot_t(grad_pre, w_node)

    sub = 512
    subs = block // sub
    holder = lax.broadcasted_iota(jnp.int32, (sub, LANES), 1) // 8
    holder = holder.astype(F32).astype(BF16)

    def backward(t, carry):
        ecot_copy(t).wait()

        def place_of(c):
            return pl.ds(pl.multiple_of(t * block + c * sub, sub), sub)

        def gathered(c):
            at = place_of(c)
            upper = upper_of(rtile_s[at, :])
            spread = picked(dot(tiles_match(rkey_s[at, :], rhalf // LANES), gtab_s[...]), upper)
            return ecot_s[at, :].astype(F32) + spread.astype(F32)

        def middle(c, grad_upd):
            at = place_of(c)
            normed = normed_s[at, :]
            scaled = grad_upd * egain_ref[...]
            inner = (
                scaled
                - jnp.mean(scaled, axis=-1, keepdims=True)
                - normed * jnp.mean(scaled * normed, axis=-1, keepdims=True)
            )
            grad_pre = paired(inner.astype(BF16), woutt_s[...]) * slope_s[at, :]
            hidden = grad_pre.astype(BF16)
            ghid_s[at, :] = hidden
            gedge_s[at, :] = grad_upd
            moved = (paired(hidden, wgeo_s[...]) * unit_s[at, :].astype(F32)).astype(BF16)
            zero = jnp.zeros_like(moved)
            return (
                jnp.where(holder == stile_s[at, :], moved, zero),
                jnp.where(holder == rtile_s[at, :], moved, zero),
            )

        upd = [None] * subs
        pairs = [None] * subs
        upd[0] = gathered(0)
        for c in range(1, subs + 1):
            if c < subs:
                upd[c] = gathered(c)
            pairs[c - 1] = middle(c - 1, upd[c - 1])
            upd[c - 1] = None
        srow = compact_row(sidx_ref[t], nodes, slots)
        rrow = ridx_ref[t]
        sgeo_s[...] += dot(
            rows_match(srow % LANES, LANES), jnp.concatenate([p[0] for p in pairs], axis=0)
        )
        rgeo_s[...] += dot(
            rows_match(rrow % LANES, LANES), jnp.concatenate([p[1] for p in pairs], axis=0)
        )
        return carry

    lax.fori_loop(0, turns, backward, 0)
    sgeo = jnp.transpose(sgeo_s[...])
    rgeo = jnp.transpose(rgeo_s[...])
    tiles = []
    for t in range(every // LANES):
        tile = sgeo[8 * t : 8 * t + 8]
        if t < nodes // LANES:
            tile = tile - rgeo[8 * t : 8 * t + 8]
        tiles.append(tile + pltpu.roll(tile, 4, 0))
    gpos = jnp.concatenate(tiles, axis=1)
    gpos = jnp.where(lax.broadcasted_iota(jnp.int32, gpos.shape, 0) < 3, gpos, 0.0)
    hi = gpos.astype(BF16).astype(F32)
    both = jnp.concatenate([hi, gpos - hi], axis=0).astype(BF16)
    amp = dot(both, phi_s[...])
    amp = amp[0:8] + amp[8:16]
    for j in range(ctrl_ref.shape[0]):
        ctrl_ref[j] = amp[0:4, j * LANES : (j + 1) * LANES]
    sum_s[...] = jnp.zeros_like(sum_s)
    for k, (inside, _) in enumerate(partners):

        @pl.when(jnp.logical_not(inside))
        def _():
            got_s[k] = jnp.zeros_like(got_s[k])

    chunks = ctrl_ref.shape[0]
    reducers = max(r for r in range(1, parts + 1) if chunks % r == 0)
    per = chunks // reducers
    def part_copy(i):
        other = others[i]
        return remote(
            ctrl_ref.at[pl.ds(jnp.minimum(other, reducers - 1) * per, per)],
            part_s.at[i],
            part_send.at[i],
            part_recv.at[i],
            other,
        )

    def all_copy(i):
        return remote(
            mine_s,
            all_s.at[pl.ds(jnp.minimum(me, reducers - 1) * per, per)],
            all_send.at[i],
            all_recv.at[i],
            others[i],
        )

    def when_reducer(device, run):
        if reducers == parts:
            run()
        else:
            pl.when(device < reducers)(run)

    def sender_step(t, carry):
        srow = compact_row(sidx_ref[t], nodes, slots)
        stile = as_columns(srow // LANES)
        second = stile >= jnp.full_like(stile, shalf // LANES)
        values = ghid_s[pl.ds(pl.multiple_of(t * block, block), block), :]
        sum_s[...] += dot(rows_match(srow % shalf, shalf), halves(values, second))
        return carry

    for i in range(parts - 1):
        when_reducer(others[i], lambda: part_copy(i).start())
    lax.fori_loop(0, turns, sender_step, 0)
    back = dot(
        jnp.concatenate(split(sum_s[shalf - NEAR * slots :, width:]), axis=1),
        wnode_s[: 2 * width],
    ).astype(BF16)
    for k in range(NEAR):
        back_s[k] = back[k * slots : (k + 1) * slots]

    def back_copy(k):
        there = NEAR - 1 - k
        return remote(
            back_s.at[k], got_s.at[there], back_send.at[k], back_recv.at[there], partners[k][1]
        )

    def reduce_mine():
        total = ctrl_ref[pl.ds(jnp.minimum(me, reducers - 1) * per, per)]
        for i in range(parts - 1):
            part_copy(i).wait_recv()
        for i in range(parts - 1):
            total = total + part_s[i]
        mine_s[...] = total
        all_s[pl.ds(jnp.minimum(me, reducers - 1) * per, per)] = total

    def edge_step(t, carry):
        at = rows_of(t)
        gedge_s[at, :] = gedge_s[at, :] + paired(ghid_s[at, :], wedge_s[...])
        return carry

    lax.fori_loop(0, turns, edge_step, 0)
    for k, (inside, _) in enumerate(partners):

        @pl.when(inside)
        def _():
            back_copy(k).start()

    when_reducer(me, reduce_mine)
    rsum_s[...] = jnp.zeros_like(rsum_s)

    def send_all():
        for i in range(parts - 1):
            all_copy(i).start()

    when_reducer(me, send_all)

    def receiver_step(t, carry):
        rrow = ridx_ref[t]
        rtile = as_columns(rrow // LANES)
        upper = rtile >= jnp.full_like(rtile, rhalf // LANES)
        values = ghid_s[pl.ds(pl.multiple_of(t * block, block), block), :]
        rsum_s[...] += dot(rows_match(rrow % rhalf, rhalf), halves(values, upper))
        return carry

    lax.fori_loop(0, turns, receiver_step, 0)
    sent = jnp.concatenate([sum_s[:, :width], sum_s[: nodes - shalf, width:]], axis=0)
    received = jnp.concatenate([rsum_s[:, :width], rsum_s[:, width:]], axis=0)
    total = gnode_s[...] + dot(
        jnp.concatenate(split(sent) + split(received), axis=1), wnode_s[...]
    )
    for k, (inside, _) in enumerate(partners):

        @pl.when(inside)
        def _():
            back_copy(NEAR - 1 - k).wait_recv()

    rows = jnp.concatenate([rows_ref[0, pl.ds(partner, 1), :] for _, partner in partners], axis=1)
    got = jnp.concatenate([got_s[k] for k in range(NEAR)], axis=0)
    out_ref[...] = total + dot(rows_match(rows, nodes), got)
    for k, (inside, _) in enumerate(partners):

        @pl.when(inside)
        def _():
            back_copy(k).wait_send()

    for i in range(parts - 1):
        when_reducer(others[i], lambda: part_copy(i).wait_send())
    when_reducer(me, lambda: [all_copy(i).wait_send() for i in range(parts - 1)] and None)
    for i in range(parts - 1):
        source = sources[i]

        def arrived():
            remote(
                mine_s,
                all_s.at[pl.ds(jnp.minimum(source, reducers - 1) * per, per)],
                all_send.at[i],
                all_recv.at[i],
                others[i],
            ).wait_recv()

        when_reducer(source, arrived)
    for j in range(chunks):
        amp_out[:, j * LANES : (j + 1) * LANES] = all_s[j][0:3]


    for k, (inside, _) in enumerate(partners):

        @pl.when(inside)
        def _():
            for copy in copies(k):
                copy.wait_send()


def layer(args, parts):
    (lat, pos, cen, amp, rows, sidx, ridx, *weights, elat, ecot, ncot) = args
    nodes, width = lat.shape
    slots = rows.shape[2]
    controls = cen.shape[1]
    every = nodes + NEAR * slots
    turns, _, block = sidx.shape
    count = turns * block
    chunks = (controls // LANES, 4, LANES)
    reducers = max(r for r in range(1, parts + 1) if chunks[0] % r == 0)
    per = (chunks[0] // reducers,) + chunks[1:]
    like = lambda x: pltpu.VMEM(x.shape, x.dtype)
    dma = lambda n: pltpu.SemaphoreType.DMA((n,))
    edge = lambda kind: pltpu.VMEM((count, width), kind)
    small = [lat, pos, cen, amp, rows, sidx, ridx, *weights]
    return pl.pallas_call(
        functools.partial(layer_kernel, parts),
        in_specs=[pl.BlockSpec(memory_space=pltpu.HBM)] * len(args),
        out_specs=[VMEM_FULL] * 3,
        out_shape=[
            jax.ShapeDtypeStruct((count, width), F32),
            jax.ShapeDtypeStruct((nodes, width), F32),
            jax.ShapeDtypeStruct((3, controls), F32),
        ],
        scratch_shapes=[like(x) for x in small]
        + [
            dma(len(small)),
            pltpu.VMEM((NEAR, slots, width), BF16),
            pltpu.VMEM((8, every), F32),
            pltpu.VMEM((NEAR, slots, width), BF16),
            pltpu.VMEM((NEAR, 8, slots), F32),
            pltpu.VMEM((NEAR, 8, slots), F32),
            pltpu.VMEM((8, nodes), F32),
            pltpu.VMEM((LANES, controls), BF16),
            pltpu.VMEM((every, controls), BF16),
            dma(NEAR),
            dma(NEAR),
            dma(NEAR),
            dma(NEAR),
            edge(BF16),
            edge(BF16),
            like(ncot),
            edge(BF16),
            pltpu.VMEM((nodes, width), F32),
            dma(turns),
            dma(turns),
            pltpu.SemaphoreType.DMA,
            pltpu.VMEM((every // 2, 2 * width), BF16),
            pltpu.VMEM((nodes // 2, 2 * width), BF16),
            pltpu.VMEM((nodes // 2, 2 * width), BF16),
            pltpu.VMEM((3 * width + LANES, width), BF16),
            pltpu.VMEM((2 * width, 2 * width), BF16),
            pltpu.VMEM((2 * width, 2 * width), BF16),
            pltpu.VMEM((2 * width, 2 * width), BF16),
            pltpu.VMEM((2 * width, 2 * width), BF16),
            edge(BF16),
            pltpu.VMEM((4 * width, width), BF16),
            edge(F32),
            edge(F32),
            edge(BF16),
            edge(BF16),
            edge(BF16),
            edge(BF16),
            pltpu.VMEM((nodes // 2, 2 * width), F32),
            pltpu.VMEM((LANES, LANES), F32),
            pltpu.VMEM((LANES, LANES), F32),
            pltpu.VMEM(chunks, F32),
            pltpu.VMEM((every // 2, 2 * width), F32),
            pltpu.VMEM((nodes // 2, 2 * width), F32),
            pltpu.VMEM((NEAR, slots, width), BF16),
            pltpu.VMEM((NEAR, slots, width), BF16),
            pltpu.VMEM((parts - 1,) + per, F32),
            pltpu.VMEM(per, F32),
            pltpu.VMEM(chunks, F32),
            dma(NEAR),
            dma(NEAR),
            dma(parts - 1),
            dma(parts - 1),
            dma(parts - 1),
            dma(parts - 1),
        ],
        compiler_params=pltpu.CompilerParams(
            collective_id=0, has_side_effects=True, vmem_limit_bytes=46 * 1024 * 1024
        ),
        name="layer",
    )(*[pltpu.with_memory_space_constraint(x, pltpu.HBM) for x in args])


def leave_kernel(*refs):
    count = (len(refs) - 1) // 2
    copies = copy_all(list(zip(refs[:count], refs[count:-1])), refs[-1])
    for copy in copies:
        copy.wait()


def leave(*values):
    return pl.pallas_call(
        leave_kernel,
        in_specs=[VMEM_FULL] * len(values),
        out_specs=[ANY] * len(values),
        out_shape=[jax.ShapeDtypeStruct(x.shape, x.dtype) for x in values],
        scratch_shapes=[pltpu.SemaphoreType.DMA((len(values),))],
        compiler_params=pltpu.CompilerParams(vmem_limit_bytes=16 * 1024 * 1024),
        name="leave",
    )(*values)


def shards(
    node_latent,
    edge_latent,
    node_cot,
    edge_cot,
    base_pos,
    centers,
    amplitudes,
    edge_in,
    edge_geo,
    edge_out,
    edge_gain,
    node_in,
    node_out,
    node_gain,
    senders,
    receivers,
    send_rows,
):
    count = senders.shape[0]
    block = 1024 if count % 1024 == 0 else 512
    grad_edges, grad_nodes, grad_controls = leave(
        *layer(
            (
                node_latent,
                base_pos,
                centers,
                amplitudes,
                send_rows,
                senders.reshape(count // block, 1, block),
                receivers.reshape(count // block, 1, block),
                edge_in,
                edge_geo,
                edge_out,
                edge_gain[None, :],
                node_in,
                node_out,
                node_gain[None, :],
                edge_latent,
                edge_cot,
                node_cot,
            ),
            lax.axis_size("dom"),
        )
    )
    return (grad_nodes, grad_edges, grad_controls)


def solution(mesh):
    split_rows = P(("groups", "dom"), None)
    in_specs = (
        split_rows,
        split_rows,
        split_rows,
        split_rows,
        P(None, ("groups", "dom")),
        P(),
        P(),
        P(),
        P(),
        P(),
        P(),
        P(),
        P(),
        P(),
        P(("groups", "dom")),
        P(("groups", "dom")),
        P(("groups", "dom"), None, None),
    )
    out_specs = (split_rows, split_rows, P("groups", None))
    return jax.shard_map(shards, mesh=mesh, in_specs=in_specs, out_specs=out_specs, check_vma=False)
```

profile of v0, /device:TPU:0, one launch (start us, length us, event | category | flops | bytes accessed | tf_op | source)
XLA Modules:
  0.0 48.7 jit_solution(322620642954501784)
XLA Ops:
  0.6 46.2 %layer.1 = (f32[6144,128]{1,0:T(8,128)S(1)}, f32[1024,128]{1,0:T(8,128)S(1)}, f32[3,2048]{1,0:T(4,128)S(1)}) custom-call(bf16[1024,128]{1,0:T(8,128)(2,1)} %refs_0_.1, f32[3,1024]{1,0:T(4,128)} %refs_1_.1, f32[3,2048]{1,0:T(4,128)} %refs_2_.1, f32[3,2048]{1,0:T(4,128)} %refs_3_.1, s32[1,16,128]{2,1,0:T(8,128)} %refs_4_.1, s32[6,1,1024]{2,1,0:T(1,128)} %bitcast.4, ...), custom_call_target="tpu_custom_call" | custom-call | tf_op jit(solution)/shard_map/layer/pallas_call | solution.py:792
  46.9 1.9 %leave.1 = (f32[6144,128]{1,0:T(8,128)}, f32[1024,128]{1,0:T(8,128)}, f32[3,2048]{1,0:T(4,128)}) custom-call(f32[6144,128]{1,0:T(8,128)S(1)} %get-tuple-element.9.refs_0_, f32[1024,128]{1,0:T(8,128)S(1)} %get-tuple-element.10.refs_1_, f32[3,2048]{1,0:T(4,128)S(1)} %get-tuple-element.11.refs_2_), custom_call_target="tpu_custom_call" | custom-call | tf_op jit(solution)/shard_map/leave/pallas_call | solution.py:873
where the time goes:
time: 49 us; the launch traced here: 48.7 us
  Pallas kernels  48.1 us (98%)
  between operations  0.65 us (1%)
    pallas_call x1, Pallas kernels, layer(): pl.pallas_call(functools.partial(layer_kernel, parts), in_specs=[pl.Block...  46.2 us
    pallas_call x1, Pallas kernels, leave(): pl.pallas_call(leave_kernel, in_specs=[VMEM_FULL] * len(values), out_spec...  1.86 us

commit v1 on v0

--- a/solution.py
+++ b/solution.py
@@ -531,7 +531,7 @@
                 joined[c] = gathered(c)
             added[c - 1] = middle(c - 1, joined[c - 1])
             joined[c - 1] = None
-        group = 4
+        group = subs
         for g in range(0, subs, group):
             row = rrow[:, g * sub : (g + group) * sub] % rhalf
             agg_s[...] += dot(rows_match(row, rhalf), jnp.concatenate(added[g : g + group], axis=0))
@@ -901,7 +901,7 @@
     send_rows,
 ):
     count = senders.shape[0]
-    block = 1024 if count % 1024 == 0 else 512
+    block = 2048 if count % 2048 == 0 else 512
     grad_edges, grad_nodes, grad_controls = leave(
         *layer(
             (

time: 49 us -> 44.4 us (0.906)
  Pallas kernels: 48.1 us -> 43.4 us
    pallas_call x1, Pallas kernels: 46.2 us -> 41.6 us  [layer(): pl.pallas_call(functools.partial(layer_kernel, parts), in_specs=[pl.Block...]
where the time goes in v1:
time: 44.4 us; the launch traced here: 44.2 us
  Pallas kernels  43.4 us (98%)
  between operations  0.81 us (2%)
    pallas_call x1, Pallas kernels, layer(): pl.pallas_call(functools.partial(layer_kernel, parts), in_specs=[pl.Block...  41.6 us
    pallas_call x1, Pallas kernels, leave(): pl.pallas_call(leave_kernel, in_specs=[VMEM_FULL] * len(values), out_spec...  1.86 us

profile of v1, /device:TPU:0, one launch (start us, length us, event | category | flops | bytes accessed | tf_op | source)
XLA Modules:
  0.0 44.2 jit_solution(11069767017291441685)
XLA Ops:
  0.6 41.6 %layer.1 = (f32[6144,128]{1,0:T(8,128)S(1)}, f32[1024,128]{1,0:T(8,128)S(1)}, f32[3,2048]{1,0:T(4,128)S(1)}) custom-call(bf16[1024,128]{1,0:T(8,128)(2,1)} %refs_0_.1, f32[3,1024]{1,0:T(4,128)} %refs_1_.1, f32[3,2048]{1,0:T(4,128)} %refs_2_.1, f32[3,2048]{1,0:T(4,128)} %refs_3_.1, s32[1,16,128]{2,1,0:T(8,128)} %refs_4_.1, s32[3,1,2048]{2,1,0:T(1,128)} %bitcast.4, ...), custom_call_target="tpu_custom_call" | custom-call | tf_op jit(solution)/shard_map/layer/pallas_call | solution.py:792
  42.2 1.9 %leave.1 = (f32[6144,128]{1,0:T(8,128)}, f32[1024,128]{1,0:T(8,128)}, f32[3,2048]{1,0:T(4,128)}) custom-call(f32[6144,128]{1,0:T(8,128)S(1)} %get-tuple-element.9.refs_0_, f32[1024,128]{1,0:T(8,128)S(1)} %get-tuple-element.10.refs_1_, f32[3,2048]{1,0:T(4,128)S(1)} %get-tuple-element.11.refs_2_), custom_call_target="tpu_custom_call" | custom-call | tf_op jit(solution)/shard_map/leave/pallas_call | solution.py:873
